TPU v7x, 32 devices: a whole 2x2x4 slice. The times are simulated.
32 devices in a mesh: rep: 1, dp: 32 (over x, y, z, core).
Axes of the slice: x: 2, y: 2, z: 4, core: 2. Of those that a mesh axis runs over, the one named last changes fastest.
Arguments:
- a: bfloat16 [32, 2, 4096, 1152], P(('rep', 'dp'))
- g: bfloat16 [32, 2, 4096, 4608], P(('rep', 'dp'))
Outputs:
- output: bfloat16 [2, 1152, 4608], P('rep')
All inputs are finite; a program needn't handle non-finite values.
Results may differ from a plain program's by a relative error of at most 0.012.
Values are sent between devices in bfloat16 or wider.
A program may use at most 2 GiB of HBM per device.

v0:
```python
import jax
import jax.numpy as jnp


def solution(mesh):
    groups = mesh.shape["rep"]

    def step(a, g):
        a, g = (t.reshape(groups, -1, *t.shape[1:]) for t in (a, g))
        sums = jnp.einsum("rsntd,rsntf->rndf", a, g, preferred_element_type=jnp.float32)
        return sums.astype(jnp.bfloat16).reshape(-1, *sums.shape[2:])

    return step
```

profile of v0, /device:TPU:0, one launch (start us, length us, event | category | flops | bytes accessed | tf_op | source)
XLA Modules:
  0.0 774.9 jit_solution(10355910536565641147)
XLA Ops:
  0.0 101.4 %fusion = f32[2,1152,4608]{2,1,0:T(8,128)} fusion(bf16[1,2,4096,4608]{3,2,1,0:T(8,128)(2,1)} %param.1, bf16[1,2,4096,1152]{3,2,1,0:T(8,128)(2,1)} %param), kind=kOutput, calls=%fused_computation | convolution fusion | flops 86973087744 | bytes 136839168 | tf_op jit(solution)/rsntd,rsntf->rndf/dot_general | solution.py:10
  101.4 673.6 %all-reduce.2 = bf16[2,1152,4608]{2,1,0:T(8,128)(2,1)} all-reduce(f32[2,1152,4608]{2,1,0:T(8,128)} %fusion), channel_id=1, replica_groups=mesh['axis_0'=32] {'axis_0'}, use_global_device_ids=true, to_apply=%add.clone | all-reduce | flops 10616832 | bytes 63700992 | tf_op jit(solution)/rsntd,rsntf->rndf/dot_general | solution.py:10
where the time goes:
time: 775 us
  blocking collectives  674 us (87%)
  matrix products  101 us (13%)
    dot_general x1, blocking collectives, step(): jnp.einsum('rsntd,rsntf->rndf', a, g, preferred_element_type=jnp.float32)  674 us
    dot_general x1, matrix products, step(): jnp.einsum('rsntd,rsntf->rndf', a, g, preferred_element_type=jnp.float32)  101 us

commit v1 on v0

v1 whole, which is shorter than its diff:
```python
import functools
import jax
import jax.numpy as jnp
from jax import lax
from jax.experimental import pallas as pl
from jax.experimental.pallas import tpu as pltpu
from jax.sharding import PartitionSpec as P

N, T, D, FF = 2, 4096, 1152, 4608
W = 256
NC = N * FF // W
PER = FF // W
HALF, QUART, EIGHTH = D // 2, D // 4, D // 8
SLAB = 256
NS = T // SLAB
K = 4
KZ = 8
LAG = 2
STAGES = 9
BF, F32 = jnp.bfloat16, jnp.float32


def kernel(a_hbm, g_hbm, res, at, stage, gbuf, acc,
           sd, k1, s1, r1, k2, sz, rz, k3, s3, rx, s4, ry,
           a_sem, g_sem, snd_d, rcv_d, snd_1, rcv_1, snd_z, rcv_z, snd_x, rcv_x, snd_y, rcv_y,
           snd_p, rcv_p, snd_g, rcv_g, snd_h, rcv_h, snd_a, rcv_a, snd_e, rcv_e):
    me = lax.axis_index("dp")
    core, z, y, x = me % 2, (me // 2) % 4, (me // 8) % 2, me // 16
    mid = (z == 1) | (z == 2)
    end = jnp.logical_not(mid)
    to_core = me + 1 - 2 * core
    to_x = me + 16 * (1 - 2 * x)
    to_y = me + 8 * (1 - 2 * y)
    to_z = me + 2 * (1 - 2 * (z % 2))
    to_m = jnp.where(mid, me + 2 * (3 - 2 * z), to_z)
    first = (to_x, to_y)
    second = (to_y, to_x)
    keep = (x, y)
    zq = z // 2

    mine = pl.multiple_of(core * HALF, HALF)
    other = pl.multiple_of((1 - core) * HALF, HALF)

    def rows_h(ab, kept=True):
        h = keep[ab] if kept else 1 - keep[ab]
        return pl.multiple_of(core * HALF + h * QUART, EIGHTH)

    def rows_q(ab, q):
        return pl.multiple_of(core * HALF + keep[ab] * QUART + q * EIGHTH, EIGHTH)

    def remote(src, dst, send, recv, dev):
        return pltpu.make_async_remote_copy(
            src_ref=src, dst_ref=dst, send_sem=send, recv_sem=recv,
            device_id={"dp": dev}, device_id_type=pl.DeviceIdType.MESH)

    def d_copy(c):
        s = c % K
        return remote(sd.at[s], res.at[c, :, pl.ds(other, HALF)], snd_d.at[s], rcv_d.at[s], to_core)

    def d_wait(c):
        s = c % K
        return remote(sd.at[s], res.at[c, :, pl.ds(mine, HALF)], snd_d.at[s], rcv_d.at[s], to_core)

    def c1(c, ab):
        s = c % K
        return remote(s1.at[s, ab], r1.at[s, ab], snd_1.at[s, ab], rcv_1.at[s, ab], first[ab])

    def cz(c, ab):
        s = c % KZ
        return remote(sz.at[s, ab], rz.at[s, ab], snd_z.at[s, ab], rcv_z.at[s, ab], to_z)

    def cx(c, ab):
        s = c % K
        return remote(s3.at[s, ab], rx.at[s, ab], snd_x.at[s, ab], rcv_x.at[s, ab], to_m)

    def cy(c, ab):
        s = c % K
        return remote(s4.at[s, ab], ry.at[s, ab], snd_y.at[s, ab], rcv_y.at[s, ab], second[ab])

    def block(c, ab, start, size):
        return res.at[c, ab, pl.ds(start, size)]

    def back(c, ab, start, size, send, recv, dev):
        ref = block(c, ab, start, size)
        s = c % KZ
        return remote(ref, ref, send.at[s, ab], recv.at[s, ab], dev)

    def cp(c, ab, q):
        return back(c, ab, rows_q(ab, q), EIGHTH, snd_p, rcv_p, to_m)

    def cg(c, ab):
        return back(c, ab, rows_q(ab, zq), EIGHTH, snd_g, rcv_g, to_z)

    def ch(c, ab):
        return back(c, ab, rows_q(ab, 1 - zq), EIGHTH, snd_h, rcv_h, to_z)

    def ca(c, ab, kept):
        return back(c, ab, rows_h(ab, kept), QUART, snd_a, rcv_a, first[ab])

    def ce(c, start):
        ref = res.at[c, :, pl.ds(start, HALF)]
        return remote(ref, ref, snd_e.at[c % K], rcv_e.at[c % K], to_core)

    def run(c, *conds):
        ok = (c >= 0) & (c < NC)
        for one in conds:
            ok = ok & one
        return pl.when(ok)

    def stage1(c):
        @run(c - LAG)
        def _():
            for ab in range(2):
                c1(c - LAG, ab).wait_send()

        @run(c)
        def _():
            s = c % K
            d_wait(c).wait_recv()
            for ab in range(2):
                cols = slice(ab * 128, ab * 128 + 128)
                away, here = rows_h(ab, False), rows_h(ab, True)
                s1[s, ab] = (acc[c % 2, pl.ds(away, QUART), cols]
                             + res[c, ab, pl.ds(away, QUART)].astype(F32)).astype(BF)
                c1(c, ab).start()
                k1[s, ab] = acc[c % 2, pl.ds(here, QUART), cols] + res[c, ab, pl.ds(here, QUART)].astype(F32)

    def stage2(c):
        @run(c - LAG, end)
        def _():
            for ab in range(2):
                cz(c - LAG, ab).wait_send()

        @run(c)
        def _():
            s = c % K
            for ab in range(2):
                c1(c, ab).wait_recv()

                @pl.when(end)
                def _():
                    sz[c % KZ, ab] = (k1[s, ab] + r1[s, ab].astype(F32)).astype(BF)
                    cz(c, ab).start()

                @pl.when(mid)
                def _():
                    k2[s, ab] = k1[s, ab] + r1[s, ab].astype(F32)

    def stage3(c):
        @run(c - LAG, mid)
        def _():
            for ab in range(2):
                cx(c - LAG, ab).wait_send()

        @run(c, mid)
        def _():
            s = c % K
            away = pl.ds(pl.multiple_of((1 - zq) * EIGHTH, EIGHTH), EIGHTH)
            here = pl.ds(pl.multiple_of(zq * EIGHTH, EIGHTH), EIGHTH)
            for ab in range(2):
                cz(c, ab).wait_recv()
                s3[s, ab] = (k2[s, ab, away] + rz[c % KZ, ab, away].astype(F32)).astype(BF)
                cx(c, ab).start()
                k3[s, ab] = k2[s, ab, here] + rz[c % KZ, ab, here].astype(F32)

    def stage4(c):
        @run(c - LAG, mid)
        def _():
            for ab in range(2):
                cy(c - LAG, ab).wait_send()

        @run(c, mid)
        def _():
            s = c % K
            for ab in range(2):
                cx(c, ab).wait_recv()
                s4[s, ab] = (k3[s, ab] + rx[s, ab].astype(F32)).astype(BF)
                cy(c, ab).start()

    def stage5(c):
        @run(c - LAG, mid)
        def _():
            for ab in range(2):
                cp(c - LAG, ab, zq).wait_send()
                cg(c - LAG, ab).wait_send()

        @run(c, mid)
        def _():
            s = c % K
            for ab in range(2):
                cy(c, ab).wait_recv()
                res[c, ab, pl.ds(rows_q(ab, zq), EIGHTH)] = (
                    s4[s, ab].astype(F32) + ry[s, ab].astype(F32)).astype(BF)
                cp(c, ab, zq).start()
                cg(c, ab).start()

    def stage6(c):
        @run(c - LAG, mid)
        def _():
            for ab in range(2):
                ch(c - LAG, ab).wait_send()
                ca(c - LAG, ab, True).wait_send()

        @run(c, mid)
        def _():
            for ab in range(2):
                cp(c, ab, 1 - zq).wait_recv()
                ch(c, ab).start()
                ca(c, ab, True).start()

    def stage7(c):
        @run(c - LAG, end)
        def _():
            for ab in range(2):
                ca(c - LAG, ab, True).wait_send()

        @run(c, end)
        def _():
            for ab in range(2):
                cg(c, ab).wait_recv()
                ch(c, ab).wait_recv()
                ca(c, ab, True).start()

    def stage8(c):
        @run(c - LAG)
        def _():
            ce(c - LAG, mine).wait_send()

        @run(c)
        def _():
            for ab in range(2):
                ca(c, ab, False).wait_recv()
            ce(c, mine).start()

    def stage9(c):
        @run(c)
        def _():
            ce(c, other).wait_recv()

    def g_copy(c):
        cols = pl.ds(pl.multiple_of((c % PER) * W, W), W)
        return pltpu.make_async_copy(g_hbm.at[c // PER, :, cols], gbuf.at[c % 2], g_sem.at[c % 2])

    def a_copy(i):
        return pltpu.make_async_copy(
            a_hbm.at[i // NS, pl.ds(pl.multiple_of((i % NS) * SLAB, SLAB), SLAB)],
            stage.at[i % K], a_sem.at[i % K])

    def transpose(i):
        a_copy(i).wait()
        at[i // NS, :, pl.ds(pl.multiple_of((i % NS) * SLAB, SLAB), SLAB)] = stage[i % K].T

        @pl.when(i + K < 2 * NS)
        def _():
            a_copy(i + K).start()

    def matmul(c):
        @run(c - LAG)
        def _():
            d_copy(c - LAG).wait_send()

        @run(c)
        def _():
            g_copy(c).wait()

            @pl.when(c + 1 < NC)
            def _():
                g_copy(c + 1).start()

            acc[c % 2] = jnp.dot(at[c // PER], gbuf[c % 2], preferred_element_type=F32)
            for ab in range(2):
                sd[c % K, ab] = acc[c % 2, pl.ds(other, HALF), ab * 128:ab * 128 + 128].astype(BF)
            d_copy(c).start()

        @pl.when(c < NS)
        def _():
            transpose(NS + c)

    for i in range(K):
        a_copy(i).start()
    g_copy(0).start()
    barrier = pltpu.get_barrier_semaphore()
    for dev in (to_core, to_x, to_y, to_z):
        pl.semaphore_signal(barrier, inc=1, device_id={"dp": dev}, device_id_type=pl.DeviceIdType.MESH)

    @pl.when(mid)
    def _():
        pl.semaphore_signal(barrier, inc=1, device_id={"dp": to_m}, device_id_type=pl.DeviceIdType.MESH)
        pl.semaphore_wait(barrier, 5)

    @pl.when(end)
    def _():
        pl.semaphore_wait(barrier, 4)

    @pl.loop(0, NS)
    def _(i):
        transpose(i)

    @pl.loop(0, NC + STAGES + LAG)
    def _(t):
        stage9(t - 9)
        stage8(t - 8)
        stage7(t - 7)
        stage6(t - 6)
        stage5(t - 5)
        stage4(t - 4)
        stage3(t - 3)
        stage2(t - 2)
        stage1(t - 1)
        matmul(t)


def place_kernel(res, out, sem):
    def copy(i):
        c, ab = i // 2, i % 2
        cols = pl.ds(pl.multiple_of((c % PER) * W + ab * 128, 128), 128)
        return pltpu.make_async_copy(res.at[c, ab], out.at[c // PER, :, cols], sem)

    @pl.loop(0, 2 * NC)
    def _(i):
        copy(i).start()

    pltpu.make_async_copy(res, res, sem).wait()


def total(a, g):
    dma = pltpu.SemaphoreType.DMA
    res = pl.pallas_call(
        kernel,
        out_shape=pltpu.VMEM((NC, 2, D, 128), BF),
        in_specs=[pl.BlockSpec(memory_space=pl.ANY)] * 2,
        out_specs=pl.BlockSpec(memory_space=pltpu.VMEM),
        scratch_shapes=[
            pltpu.VMEM((N, D, T), BF),
            pltpu.VMEM((K, SLAB, D), BF),
            pltpu.VMEM((2, T, W), BF),
            pltpu.VMEM((2, D, W), F32),
            pltpu.VMEM((K, 2, HALF, 128), BF),
            pltpu.VMEM((K, 2, QUART, 128), F32),
            pltpu.VMEM((K, 2, QUART, 128), BF),
            pltpu.VMEM((K, 2, QUART, 128), BF),
            pltpu.VMEM((K, 2, QUART, 128), F32),
            pltpu.VMEM((KZ, 2, QUART, 128), BF),
            pltpu.VMEM((KZ, 2, QUART, 128), BF),
            pltpu.VMEM((K, 2, EIGHTH, 128), F32),
            pltpu.VMEM((K, 2, EIGHTH, 128), BF),
            pltpu.VMEM((K, 2, EIGHTH, 128), BF),
            pltpu.VMEM((K, 2, EIGHTH, 128), BF),
            pltpu.VMEM((K, 2, EIGHTH, 128), BF),
            dma((K,)), dma((2,)),
            dma((K,)), dma((K,)),
        ] + [dma((K, 2))] * 2 + [dma((KZ, 2))] * 2 + [dma((K, 2))] * 4 + [dma((KZ, 2))] * 8 + [dma((K,)), dma((K,))],
        compiler_params=pltpu.CompilerParams(
            collective_id=0, has_side_effects=True, vmem_limit_bytes=VL),
        name="sum_tiles",
    )(a, g)
    return pl.pallas_call(
        place_kernel,
        out_shape=jax.ShapeDtypeStruct((N, D, FF), BF),
        in_specs=[pl.BlockSpec(memory_space=pltpu.VMEM)],
        out_specs=pl.BlockSpec(memory_space=pl.ANY),
        scratch_shapes=[pltpu.SemaphoreType.DMA],
        compiler_params=pltpu.CompilerParams(vmem_limit_bytes=VL2),
        name="place",
    )(res)


VL = 42 * 2**20
VL2 = 30 * 2**20


def solution(mesh):
    def body(a, g):
        return total(a[0], g[0])

    return jax.shard_map(body, mesh=mesh, in_specs=(P(("rep", "dp")), P(("rep", "dp"))),
                         out_specs=P("rep"), check_vma=False)
```

time: 775 us -> 204 us (0.26)
  blocking collectives: 674 us -> 0 us
  Pallas kernels: 0 us -> 204 us
  matrix products: 101 us -> 0 us
    dot_general x1 -> x0, blocking collectives: 674 us -> none  [step(): jnp.einsum('rsntd,rsntf->rndf', a, g, preferred_element_type=jnp.float32)]
    pallas_call x0 -> x2, Pallas kernels: none -> 204 us  [the longest x1 197 us: total(): pl.pallas_call(kernel, out_shape=pltpu.VMEM((NC, 2, D, 128), BF), in_spec...]
    dot_general x1 -> x0, matrix products: 101 us -> none  [step(): jnp.einsum('rsntd,rsntf->rndf', a, g, preferred_element_type=jnp.float32)]
where the time goes in v1:
time: 204 us
  Pallas kernels  204 us (100%)
    pallas_call x1, Pallas kernels, total(): pl.pallas_call(kernel, out_shape=pltpu.VMEM((NC, 2, D, 128), BF), in_spec...  197 us
    pallas_call x1, Pallas kernels, total(): pl.pallas_call(place_kernel, out_shape=jax.ShapeDtypeStruct((N, D, FF), B...  7.15 us

profile of v1, /device:TPU:0, one launch (start us, length us, event | category | flops | bytes accessed | tf_op | source)
XLA Modules:
  0.0 203.8 jit_solution(11913081176952794562)
XLA Ops:
  0.0 196.6 %sum_tiles.1.res = bf16[36,2,1152,128]{3,2,1,0:T(8,128)(2,1)S(1)} custom-call(bf16[2,4096,1152]{2,1,0:T(8,128)(2,1)} %bitcast.2, bf16[2,4096,4608]{2,1,0:T(8,128)(2,1)} %bitcast.1.g_hbm), custom_call_target="tpu_custom_call" | custom-call | tf_op jit(solution)/shard_map/sum_tiles/pallas_call | solution.py:328
  196.6 7.1 %place.1 = bf16[2,1152,4608]{2,1,0:T(8,128)(2,1)} custom-call(bf16[36,2,1152,128]{3,2,1,0:T(8,128)(2,1)S(1)} %sum_tiles.1.res), custom_call_target="tpu_custom_call" | custom-call | tf_op jit(solution)/shard_map/place/pallas_call | solution.py:357

commit v2 on v0

v2 whole, which is shorter than its diff:
```python
import jax
import jax.numpy as jnp
from jax import lax
from jax.experimental import pallas as pl
from jax.experimental.pallas import tpu as pltpu
from jax.sharding import PartitionSpec as P

N, T, D, FF = 2, 4096, 1152, 4608
W = 256
NC = N * FF // W
PER = FF // W
HALF, QUART = D // 2, D // 4
OUT, IN = 64, 80
SIDE = OUT + IN
SLAB = 256
NS = T // SLAB
K, KR = 4, 8
LAG = 2
AS = 3
OFF = {1: 2, 2: 3, 3: 4, 4: 6, 5: 9, 6: 9, 7: 10, 8: 11, "A": 15, "B": 22}
ORDER = (5, 1, "A", "M", 4, 7, 8, 3, 2, "B", 6)
BF, F32 = jnp.bfloat16, jnp.float32
DMA = pltpu.SemaphoreType.DMA

BUFFERS = dict(
    at=pltpu.VMEM((N, D, T), BF),
    stage=pltpu.VMEM((AS, SLAB, D), BF),
    gbuf=pltpu.VMEM((2, T, W), BF),
    acc=pltpu.VMEM((2, D, W), F32),
    sd=pltpu.VMEM((K, 2, HALF, 128), BF),
    k1=pltpu.VMEM((K, 2, QUART, 128), F32),
    s1=pltpu.VMEM((K, 2, QUART, 128), BF),
    r1=pltpu.VMEM((KR, 2, QUART, 128), BF),
    k2=pltpu.VMEM((K, 2, QUART, 128), F32),
    sz=pltpu.VMEM((K, 2, QUART - OUT, 128), BF),
    rz=pltpu.VMEM((KR, 2, QUART - OUT, 128), BF),
    ke=pltpu.VMEM((KR, 2, OUT, 128), F32),
    k3=pltpu.VMEM((K, 2, SIDE, 128), F32),
    s3=pltpu.VMEM((K, 2, SIDE, 128), BF),
    rx=pltpu.VMEM((KR, 2, SIDE, 128), BF),
    sc=pltpu.VMEM((K, 2, OUT, 128), BF),
    rc=pltpu.VMEM((KR, 2, OUT, 128), BF),
    s4=pltpu.VMEM((KR, 2, IN, 128), BF),
    ry=pltpu.VMEM((KR, 2, IN, 128), BF),
)
LINKS = ("1", "z", "x", "c", "y", "g1", "g2", "p1", "p0", "q0", "a")
SEMS = dict(a_sem=DMA((AS,)), g_sem=DMA((2,)),
            snd_d=DMA((K,)), rcv_d=DMA((KR,)), snd_e=DMA((K,)), rcv_e=DMA((NC,)))
for link in LINKS:
    SEMS["snd_" + link] = DMA((K, 2))
    SEMS["rcv_" + link] = DMA((KR if link in ("1", "z", "x", "c", "y") else NC, 2))
SCRATCH = {**BUFFERS, **SEMS}


def kernel(a_hbm, g_hbm, res, *scratch):
    r = dict(zip(SCRATCH, scratch))
    me = lax.axis_index("dp")
    core, z, y, x = me % 2, (me // 2) % 4, (me // 8) % 2, me // 16
    mid = (z == 1) | (z == 2)
    end = jnp.logical_not(mid)
    to_core = me + 1 - 2 * core
    to_x = me + 16 * (1 - 2 * x)
    to_y = me + 8 * (1 - 2 * y)
    to_z = me + 2 * (1 - 2 * (z % 2))
    to_m = jnp.where(mid, me + 2 * (3 - 2 * z), to_z)
    first = (to_x, to_y)
    second = (to_y, to_x)
    keep = (x, y)
    side = z // 2

    def aligned(v):
        return pl.multiple_of(v, 16)

    mine = aligned(core * HALF)
    other = aligned((1 - core) * HALF)
    out_at = side * (QUART - OUT)
    in_at = OUT + side * IN
    far_at = (1 - side) * SIDE
    up_at = (1 - side) * OUT

    def quarter(ab, kept=True):
        return aligned(core * HALF + (keep[ab] if kept else 1 - keep[ab]) * QUART)

    def rows(v, size):
        return pl.ds(aligned(v), size)

    def remote(src, dst, link, c, ab, dev):
        snd, rcv = r["snd_" + link], r["rcv_" + link]
        ks, kr = snd.shape[0], rcv.shape[0]
        at = () if ab is None else (ab,)
        return pltpu.make_async_remote_copy(
            src_ref=src, dst_ref=dst, send_sem=snd.at[(c % ks,) + at], recv_sem=rcv.at[(c % kr,) + at],
            device_id={"dp": dev}, device_id_type=pl.DeviceIdType.MESH)

    def d_copy(c, start):
        return remote(r["sd"].at[c % K], res.at[c, :, pl.ds(start, HALF)], "d", c, None, to_core)

    def c1(c, ab):
        return remote(r["s1"].at[c % K, ab], r["r1"].at[c % KR, ab], "1", c, ab, first[ab])

    def cz(c, ab):
        return remote(r["sz"].at[c % K, ab], r["rz"].at[c % KR, ab], "z", c, ab, to_z)

    def cx(c, ab):
        return remote(r["s3"].at[c % K, ab], r["rx"].at[c % KR, ab], "x", c, ab, to_m)

    def cc(c, ab):
        return remote(r["sc"].at[c % K, ab], r["rc"].at[c % KR, ab], "c", c, ab, to_z)

    def cy(c, ab, size):
        return remote(r["s4"].at[c % KR, ab, pl.ds(0, size)], r["ry"].at[c % KR, ab, pl.ds(0, size)],
                      "y", c, ab, second[ab])

    def part(link, c, ab, v, size, dev):
        ref = res.at[c, ab, rows(quarter(ab) + v, size)]
        return remote(ref, ref, link, c, ab, dev)

    def g1(c, ab):
        return part("g1", c, ab, in_at, IN, to_z)

    def g2(c, ab):
        return part("g2", c, ab, far_at, SIDE, to_z)

    def p1(c, ab, s=None):
        return part("p1", c, ab, in_at if s is None else OUT + s * IN, IN, to_m)

    def p0(c, ab, s=None):
        return part("p0", c, ab, out_at if s is None else s * (QUART - OUT), OUT, to_m)

    def q0(c, ab):
        return part("q0", c, ab, out_at, OUT, to_z)

    def ca(c, ab, kept=True):
        ref = res.at[c, ab, pl.ds(quarter(ab, kept), QUART)]
        return remote(ref, ref, "a", c, ab, first[ab])

    def ce(c, start):
        ref = res.at[c, :, pl.ds(start, HALF)]
        return remote(ref, ref, "e", c, None, to_core)

    sent = []

    def settle(c, where, *copies):
        sent.append((where, copies))

        @pl.when((c >= LAG) & (c < NC) & where)
        def _():
            for copy in copies:
                for ab in range(2):
                    copy(c - LAG, ab).wait_send()

    def run(c, where):
        return pl.when((c >= 0) & (c < NC) & where)

    def f32(ref):
        return ref.astype(F32)

    def stage1(c):
        settle(c, True, c1)

        @run(c, True)
        def _():
            d_copy(c, mine).wait_recv()
            for ab in range(2):
                cols = slice(ab * 128, ab * 128 + 128)
                away, here = pl.ds(quarter(ab, False), QUART), pl.ds(quarter(ab), QUART)
                r["s1"][c % K, ab] = (r["acc"][c % 2, away, cols] + f32(res[c, ab, away])).astype(BF)
                c1(c, ab).start()
                r["k1"][c % K, ab] = r["acc"][c % 2, here, cols] + f32(res[c, ab, here])

    def stage2(c):
        settle(c, end, cz)

        @run(c, True)
        def _():
            for ab in range(2):
                c1(c, ab).wait_recv()

                @pl.when(end)
                def _():
                    up, own = rows(up_at, QUART - OUT), rows(out_at, OUT)
                    r["sz"][c % K, ab] = (r["k1"][c % K, ab, up] + f32(r["r1"][c % KR, ab, up])).astype(BF)
                    cz(c, ab).start()
                    r["ke"][c % KR, ab] = r["k1"][c % K, ab, own] + f32(r["r1"][c % KR, ab, own])

                @pl.when(mid)
                def _():
                    r["k2"][c % K, ab] = r["k1"][c % K, ab] + f32(r["r1"][c % KR, ab])

    def stage3(c):
        settle(c, mid, cx)

        @run(c, mid)
        def _():
            for ab in range(2):
                cz(c, ab).wait_recv()
                rz, k2, k3 = r["rz"], r["k2"], r["k3"]
                r["s3"][c % K, ab] = (k2[c % K, ab, rows(far_at, SIDE)]
                                      + f32(rz[c % KR, ab, rows((1 - side) * IN, SIDE)])).astype(BF)
                cx(c, ab).start()
                k3[c % K, ab, 0:IN] = k2[c % K, ab, rows(in_at, IN)] + f32(rz[c % KR, ab, rows(side * SIDE, IN)])
                k3[c % K, ab, IN:SIDE] = k2[c % K, ab, rows(out_at, OUT)]

    def stage4(c):
        settle(c, mid, cc, lambda c, ab: cy(c, ab, IN))

        @run(c, mid)
        def _():
            for ab in range(2):
                cx(c, ab).wait_recv()
                k3, rx = r["k3"], r["rx"]
                r["sc"][c % K, ab] = (k3[c % K, ab, IN:SIDE]
                                      + f32(rx[c % KR, ab, rows(side * IN, OUT)])).astype(BF)
                cc(c, ab).start()
                r["s4"][c % KR, ab] = (k3[c % K, ab, 0:IN]
                                       + f32(rx[c % KR, ab, rows((1 - side) * OUT, IN)])).astype(BF)
                cy(c, ab, IN).start()

    def stage5(c):
        settle(c, end, lambda c, ab: cy(c, ab, OUT))

        @run(c, end)
        def _():
            for ab in range(2):
                cc(c, ab).wait_recv()
                r["s4"][c % KR, ab, 0:OUT] = (r["ke"][c % KR, ab] + f32(r["rc"][c % KR, ab])).astype(BF)
                cy(c, ab, OUT).start()

    def stage6(c):
        settle(c, mid, g1, p1)
        settle(c, end, q0)

        def last(ab, v, size):
            cy(c, ab, size).wait_recv()
            res[c, ab, rows(quarter(ab) + v, size)] = (
                f32(r["s4"][c % KR, ab, 0:size]) + f32(r["ry"][c % KR, ab, 0:size])).astype(BF)

        @run(c, mid)
        def _():
            for ab in range(2):
                last(ab, in_at, IN)
                p1(c, ab).start()
                g1(c, ab).start()

        @run(c, end)
        def _():
            for ab in range(2):
                last(ab, out_at, OUT)
                q0(c, ab).start()

    def stage7(c):
        settle(c, mid, p0)

        @run(c, mid)
        def _():
            for ab in range(2):
                q0(c, ab).wait_recv()
                p0(c, ab).start()

    def stage8(c):
        settle(c, mid, g2)

        @run(c, mid)
        def _():
            for ab in range(2):
                p1(c, ab, 1 - side).wait_recv()
                p0(c, ab, 1 - side).wait_recv()
                g2(c, ab).start()

    def stage_a(c):
        settle(c, True, ca)

        @run(c, True)
        def _():
            for ab in range(2):
                @pl.when(end)
                def _():
                    g1(c, ab).wait_recv()
                    g2(c, ab).wait_recv()

                ca(c, ab).start()

    def stage_b(c):
        @pl.when((c >= LAG) & (c < NC))
        def _():
            ce(c - LAG, mine).wait_send()

        @run(c, True)
        def _():
            for ab in range(2):
                ca(c, ab, False).wait_recv()
            ce(c, mine).start()

    def g_copy(c):
        cols = pl.ds(pl.multiple_of((c % PER) * W, W), W)
        return pltpu.make_async_copy(g_hbm.at[c // PER, :, cols], r["gbuf"].at[c % 2], r["g_sem"].at[c % 2])

    def a_copy(i):
        return pltpu.make_async_copy(
            a_hbm.at[i // NS, pl.ds(pl.multiple_of((i % NS) * SLAB, SLAB), SLAB)],
            r["stage"].at[i % AS], r["a_sem"].at[i % AS])

    def transpose(i):
        a_copy(i).wait()
        r["at"][i // NS, :, pl.ds(pl.multiple_of((i % NS) * SLAB, SLAB), SLAB)] = r["stage"][i % AS].T

        @pl.when(i + AS < 2 * NS)
        def _():
            a_copy(i + AS).start()

    def matmul(c):
        @pl.when((c >= LAG) & (c < NC))
        def _():
            d_copy(c - LAG, other).wait_send()

        @run(c, True)
        def _():
            g_copy(c).wait()

            @pl.when(c + 1 < NC)
            def _():
                g_copy(c + 1).start()

            r["acc"][c % 2] = jnp.dot(r["at"][c // PER], r["gbuf"][c % 2], preferred_element_type=F32)
            for ab in range(2):
                cols = slice(ab * 128, ab * 128 + 128)
                r["sd"][c % K, ab] = r["acc"][c % 2, pl.ds(other, HALF), cols].astype(BF)
            d_copy(c, other).start()

        @pl.when(c < NS)
        def _():
            transpose(NS + c)

    for i in range(AS):
        a_copy(i).start()
    g_copy(0).start()
    barrier = pltpu.get_barrier_semaphore()

    def greet(dev):
        pl.semaphore_signal(barrier, inc=1, device_id={"dp": dev}, device_id_type=pl.DeviceIdType.MESH)

    for dev in (to_core, to_x, to_y, to_z):
        greet(dev)

    @pl.when(mid)
    def _():
        greet(to_m)
        pl.semaphore_wait(barrier, 5)

    @pl.when(end)
    def _():
        pl.semaphore_wait(barrier, 4)

    @pl.loop(0, NS)
    def _(i):
        transpose(i)

    steps = {1: stage1, 2: stage2, 3: stage3, 4: stage4, 5: stage5, 6: stage6, 7: stage7, 8: stage8,
             "A": stage_a, "B": stage_b, "M": matmul}

    @pl.loop(0, NC + max(OFF.values()))
    def _(t):
        for name in ORDER:
            steps[name](t - OFF.get(name, 0))

    for c in range(NC - LAG, NC):
        for where, copies in sent:
            @pl.when(where)
            def _():
                for copy in copies:
                    for ab in range(2):
                        copy(c, ab).wait_send()
        d_copy(c, other).wait_send()
        ce(c, mine).wait_send()

    @pl.loop(0, NC)
    def _(c):
        ce(c, other).wait_recv()


def place_kernel(res, out, sem):
    def copy(i):
        c, ab = i // 2, i % 2
        cols = pl.ds(pl.multiple_of((c % PER) * W + ab * 128, 128), 128)
        return pltpu.make_async_copy(res.at[c, ab], out.at[c // PER, :, cols], sem)

    @pl.loop(0, 2 * NC)
    def _(i):
        copy(i).start()

    pltpu.make_async_copy(res, res, sem).wait()


def total(a, g):
    res = pl.pallas_call(
        kernel,
        out_shape=pltpu.VMEM((NC, 2, D, 128), BF),
        in_specs=[pl.BlockSpec(memory_space=pl.ANY)] * 2,
        out_specs=pl.BlockSpec(memory_space=pltpu.VMEM),
        scratch_shapes=list(SCRATCH.values()),
        compiler_params=pltpu.CompilerParams(
            collective_id=0, has_side_effects=True, vmem_limit_bytes=42 * 2**20),
        name="sum_tiles",
    )(a, g)
    return pl.pallas_call(
        place_kernel,
        out_shape=jax.ShapeDtypeStruct((N, D, FF), BF),
        in_specs=[pl.BlockSpec(memory_space=pltpu.VMEM)],
        out_specs=pl.BlockSpec(memory_space=pl.ANY),
        scratch_shapes=[pltpu.SemaphoreType.DMA],
        compiler_params=pltpu.CompilerParams(vmem_limit_bytes=30 * 2**20),
        name="place",
    )(res)


def solution(mesh):
    def body(a, g):
        return total(a[0], g[0])

    return jax.shard_map(body, mesh=mesh, in_specs=(P(("rep", "dp")), P(("rep", "dp"))),
                         out_specs=P("rep"), check_vma=False)
```

time: 775 us -> 189 us (0.24)
  blocking collectives: 674 us -> 0 us
  Pallas kernels: 0 us -> 189 us
  matrix products: 101 us -> 0 us
    dot_general x1 -> x0, blocking collectives: 674 us -> none  [step(): jnp.einsum('rsntd,rsntf->rndf', a, g, preferred_element_type=jnp.float32)]
    pallas_call x0 -> x2, Pallas kernels: none -> 189 us  [the longest x1 182 us: total(): pl.pallas_call(kernel, out_shape=pltpu.VMEM((NC, 2, D, 128), BF), in_spec...]
    dot_general x1 -> x0, matrix products: 101 us -> none  [step(): jnp.einsum('rsntd,rsntf->rndf', a, g, preferred_element_type=jnp.float32)]
where the time goes in v2:
time: 189 us
  Pallas kernels  189 us (100%)
    pallas_call x1, Pallas kernels, total(): pl.pallas_call(kernel, out_shape=pltpu.VMEM((NC, 2, D, 128), BF), in_spec...  182 us
    pallas_call x1, Pallas kernels, total(): pl.pallas_call(place_kernel, out_shape=jax.ShapeDtypeStruct((N, D, FF), B...  7.15 us

profile of v2, /device:TPU:0, one launch (start us, length us, event | category | flops | bytes accessed | tf_op | source)
XLA Modules:
  0.0 188.9 jit_solution(11491786138247459621)
XLA Ops:
  0.0 181.7 %sum_tiles.1.res = bf16[36,2,1152,128]{3,2,1,0:T(8,128)(2,1)S(1)} custom-call(bf16[2,4096,1152]{2,1,0:T(8,128)(2,1)} %bitcast.2, bf16[2,4096,4608]{2,1,0:T(8,128)(2,1)} %bitcast.1.g_hbm), custom_call_target="tpu_custom_call" | custom-call | tf_op jit(solution)/shard_map/sum_tiles/pallas_call | solution.py:395
  181.7 7.1 %place.1 = bf16[2,1152,4608]{2,1,0:T(8,128)(2,1)} custom-call(bf16[36,2,1152,128]{3,2,1,0:T(8,128)(2,1)S(1)} %sum_tiles.1.res), custom_call_target="tpu_custom_call" | custom-call | tf_op jit(solution)/shard_map/place/pallas_call | solution.py:405

commit v3 on v2

--- a/solution.py
+++ b/solution.py
@@ -17,8 +17,8 @@
 K, KR = 4, 8
 LAG = 2
 AS = 3
-OFF = {1: 2, 2: 3, 3: 4, 4: 6, 5: 9, 6: 9, 7: 10, 8: 11, "A": 15, "B": 22}
-ORDER = (5, 1, "A", "M", 4, 7, 8, 3, 2, "B", 6)
+OFF = {1: 1, 2: 3, 3: 4, 4: 5, 5: 7, 6: 8, 7: 9, 8: 10, "A": 13, "B": 20}
+ORDER = (5, "A", 7, 8, 6, "B", 2, "M0", 3, 1, 4, "M1")
 BF, F32 = jnp.bfloat16, jnp.float32
 DMA = pltpu.SemaphoreType.DMA
 
@@ -26,7 +26,7 @@
     at=pltpu.VMEM((N, D, T), BF),
     stage=pltpu.VMEM((AS, SLAB, D), BF),
     gbuf=pltpu.VMEM((2, T, W), BF),
-    acc=pltpu.VMEM((2, D, W), F32),
+    acc=pltpu.VMEM((3, HALF, W), F32),
     sd=pltpu.VMEM((K, 2, HALF, 128), BF),
     k1=pltpu.VMEM((K, 2, QUART, 128), F32),
     s1=pltpu.VMEM((K, 2, QUART, 128), BF),
@@ -163,10 +163,12 @@
             d_copy(c, mine).wait_recv()
             for ab in range(2):
                 cols = slice(ab * 128, ab * 128 + 128)
-                away, here = pl.ds(quarter(ab, False), QUART), pl.ds(quarter(ab), QUART)
-                r["s1"][c % K, ab] = (r["acc"][c % 2, away, cols] + f32(res[c, ab, away])).astype(BF)
+                h = keep[ab]
+                away, here = rows((1 - h) * QUART, QUART), rows(h * QUART, QUART)
+                r["s1"][c % K, ab] = (r["acc"][c % 3, away, cols]
+                                      + f32(res[c, ab, pl.ds(quarter(ab, False), QUART)])).astype(BF)
                 c1(c, ab).start()
-                r["k1"][c % K, ab] = r["acc"][c % 2, here, cols] + f32(res[c, ab, here])
+                r["k1"][c % K, ab] = r["acc"][c % 3, here, cols] + f32(res[c, ab, pl.ds(quarter(ab), QUART)])
 
     def stage2(c):
         settle(c, end, cz)
@@ -308,7 +310,10 @@
         def _():
             a_copy(i + AS).start()
 
-    def matmul(c):
+    def product(c, start):
+        return jnp.dot(r["at"][c // PER, pl.ds(start, HALF)], r["gbuf"][c % 2], preferred_element_type=F32)
+
+    def matmul0(c):
         @pl.when((c >= LAG) & (c < NC))
         def _():
             d_copy(c - LAG, other).wait_send()
@@ -321,11 +326,15 @@
             def _():
                 g_copy(c + 1).start()
 
-            r["acc"][c % 2] = jnp.dot(r["at"][c // PER], r["gbuf"][c % 2], preferred_element_type=F32)
-            for ab in range(2):
-                cols = slice(ab * 128, ab * 128 + 128)
-                r["sd"][c % K, ab] = r["acc"][c % 2, pl.ds(other, HALF), cols].astype(BF)
+            out = product(c, other).astype(BF)
+            for ab in range(2):
+                r["sd"][c % K, ab] = out[:, ab * 128:ab * 128 + 128]
             d_copy(c, other).start()
+
+    def matmul1(c):
+        @run(c, True)
+        def _():
+            r["acc"][c % 3] = product(c, mine)
 
         @pl.when(c < NS)
         def _():
@@ -356,7 +365,7 @@
         transpose(i)
 
     steps = {1: stage1, 2: stage2, 3: stage3, 4: stage4, 5: stage5, 6: stage6, 7: stage7, 8: stage8,
-             "A": stage_a, "B": stage_b, "M": matmul}
+             "A": stage_a, "B": stage_b, "M0": matmul0, "M1": matmul1}
 
     @pl.loop(0, NC + max(OFF.values()))
     def _(t):

time: 189 us -> 186 us (0.984)
  Pallas kernels: 189 us -> 186 us
    pallas_call x1, Pallas kernels: 182 us -> 179 us  [total(): pl.pallas_call(kernel, out_shape=pltpu.VMEM((NC, 2, D, 128), BF), in_spec...]
where the time goes in v3:
time: 186 us
  Pallas kernels  186 us (100%)
    pallas_call x1, Pallas kernels, total(): pl.pallas_call(kernel, out_shape=pltpu.VMEM((NC, 2, D, 128), BF), in_spec...  179 us
    pallas_call x1, Pallas kernels, total(): pl.pallas_call(place_kernel, out_shape=jax.ShapeDtypeStruct((N, D, FF), B...  7.15 us

profile of v3, /device:TPU:0, one launch (start us, length us, event | category | flops | bytes accessed | tf_op | source)
XLA Modules:
  0.0 185.9 jit_solution(912767507444608947)
XLA Ops:
  0.0 178.8 %sum_tiles.1.res = bf16[36,2,1152,128]{3,2,1,0:T(8,128)(2,1)S(1)} custom-call(bf16[2,4096,1152]{2,1,0:T(8,128)(2,1)} %bitcast.2, bf16[2,4096,4608]{2,1,0:T(8,128)(2,1)} %bitcast.1.g_hbm), custom_call_target="tpu_custom_call" | custom-call | tf_op jit(solution)/shard_map/sum_tiles/pallas_call | solution.py:404
  178.8 7.1 %place.1 = bf16[2,1152,4608]{2,1,0:T(8,128)(2,1)} custom-call(bf16[36,2,1152,128]{3,2,1,0:T(8,128)(2,1)S(1)} %sum_tiles.1.res), custom_call_target="tpu_custom_call" | custom-call | tf_op jit(solution)/shard_map/place/pallas_call | solution.py:414
